TPU v7x, 32 devices: a whole 2x2x4 slice. The times are simulated.
32 devices in a mesh: dp: 16 (over z, x, core), tensor: 2 (over y).
Axes of the slice: x: 2, y: 2, z: 4, core: 2. Of those that a mesh axis runs over, the one named last changes fastest.
Arguments:
- hidden: bfloat16 [5120, 18432], P('dp', 'tensor'), may hold values from -6 to 6
- fixed_down_weight: bfloat16 [18432, 4608], P('tensor', 'dp'), may hold values from -4 to 4
- lowrank_factor_b: bfloat16 [18432, 16], P('tensor'), may hold values from -0.046875 to 0.046875
- lowrank_factor_a: bfloat16 [16, 4608], P(None, 'dp'), may hold values from -1.5 to 1.5
- magnitude: float32 [4608], P('tensor'), may hold values from 0.5 to 2
- cotangent: bfloat16 [5120, 4608], P('dp', 'tensor'), may hold values from -0.083496094 to 0.083496094
Outputs:
- mixed: bfloat16 [5120, 4608], P('dp', 'tensor')
- gradient_column_scale: float32 [4608], P(('tensor', 'dp'))
- gradient_factor_a: float32 [16, 4608], P(None, ('tensor', 'dp'))
- gradient_factor_b: float32 [18432, 16], P(('tensor', 'dp'))
All inputs are finite; a program needn't handle non-finite values.
Results may differ from a plain program's by a relative error of at most 0.0054.
Values may be sent and summed in bfloat16 or wider, within the bound.
No kernel may reach another device: no remote copies, remote signals or barrier semaphores. Data moves between devices by JAX's collectives and lax.ppermute only.
A program may use at most 192 MiB of HBM per device.

v0:
```python
import jax
import jax.numpy as jnp
from jax import lax
from jax.sharding import PartitionSpec as P


def body(hidden, fixed_down_weight, lowrank_factor_b, lowrank_factor_a, magnitude, cotangent):
    out_cols = magnitude.shape[0]
    own = lax.axis_index("tensor")
    lowrank_portion = jnp.dot(hidden, lowrank_factor_b, preferred_element_type=jnp.float32)
    combined_weight = fixed_down_weight.astype(jnp.float32) + jnp.dot(
        lowrank_factor_b, lowrank_factor_a, preferred_element_type=jnp.float32
    )
    local_sq = jnp.sum(combined_weight * combined_weight, axis=0)
    low_full, block_sq = lax.psum((lowrank_portion, local_sq), "tensor")
    col_sq = lax.all_gather(block_sq, "dp", axis=0, tiled=True)
    sq_len = 1
    weight_shape = (1, 1)
    squares = jnp.zeros((sq_len,), jnp.float32)
    full_w = jnp.zeros(weight_shape, jnp.bfloat16)
    w_piece = lax.all_gather(fixed_down_weight, "dp", axis=1, tiled=True)
    factor_a_slice = lax.all_gather(lowrank_factor_a, "dp", axis=1, tiled=True)
    products = jnp.dot(hidden, w_piece, preferred_element_type=jnp.float32)
    full_a = factor_a_slice
    products, squares, full_a, full_w = (products, squares, full_a, full_w)
    column_norm_values = jnp.sqrt(col_sq + 1e-06)
    own_norms = lax.dynamic_slice_in_dim(column_norm_values, own * out_cols, out_cols, 0)
    scale = magnitude / own_norms
    lowrank_block_update = low_full.astype(jnp.bfloat16)
    summed = lax.psum_scatter(products, "tensor", scatter_dimension=1, tiled=True)
    own_a = lax.dynamic_slice_in_dim(full_a, own * out_cols, out_cols, 1)
    prenorm_output = summed + jnp.dot(
        lowrank_block_update, own_a, preferred_element_type=jnp.float32
    )
    mixed = (prenorm_output * scale).astype(jnp.bfloat16)
    cot = cotangent.astype(jnp.float32)
    mag_part = jnp.sum(cot * prenorm_output, axis=0) / own_norms
    prenorm_gradient_b = (cot * scale).astype(jnp.bfloat16)
    factor_a_portion = jnp.dot(
        lowrank_block_update.T, prenorm_gradient_b, preferred_element_type=jnp.float32
    )
    back_part = jnp.dot(prenorm_gradient_b, own_a.T, preferred_element_type=jnp.float32)
    backward_factor_b = lax.psum(back_part, "tensor").astype(jnp.bfloat16)
    b_part = jnp.dot(hidden.T, backward_factor_b, preferred_element_type=jnp.float32)
    gradient_column_scale, gradient_factor_b = (
        lax.psum_scatter(mag_part, "dp", scatter_dimension=0, tiled=True),
        lax.psum_scatter(b_part, "dp", scatter_dimension=0, tiled=True),
    )
    gradient_factor_a = lax.psum_scatter(factor_a_portion, "dp", scatter_dimension=1, tiled=True)
    return (mixed, gradient_column_scale, gradient_factor_a, gradient_factor_b)


def solution(mesh):
    return jax.shard_map(
        body,
        mesh=mesh,
        in_specs=(
            P("dp", "tensor"),
            P("tensor", "dp"),
            P("tensor", None),
            P(None, "dp"),
            P("tensor"),
            P("dp", "tensor"),
        ),
        out_specs=(
            P("dp", "tensor"),
            P(("tensor", "dp")),
            P(None, ("tensor", "dp")),
            P(("tensor", "dp"), None),
        ),
        check_vma=False,
    )
```

profile of v0, /device:TPU:0, one launch (start us, length us, event | category | flops | bytes accessed | tf_op | source)
XLA Modules:
  0.0 711.5 jit_solution(8600215113139559798)
XLA Ops:
  7.2 0.0 copy-start
  7.2 0.0 copy-start.4
  7.2 0.0 copy-start.2
  7.2 0.0 all-gather.3.cloned.1.call-start
  7.2 0.7 all-gather.3.cloned.1.call-update
  7.9 0.0 reduce-scatter.10.cloned.1.call-start
  8.0 0.0 copy-done.2
  8.0 24.5 %all-gather = bf16[16,288,16]{1,2,0:T(8,128)(2,1)S(1)} all-gather(bf16[1,288,16]{1,2,0:T(8,128)(2,1)S(1)} %bitcast.24), channel_id=1, replica_groups=mesh['dp'=16,'tensor'=2] {'dp'}, dimensions={0}, use_global_device_ids=true | all-gather | bytes 156672 | tf_op jit(solution)/shard_map/all_gather | solution.py:22
  32.6 0.2 reshape.13
  32.8 0.0 copy-done.4
  32.8 0.6 fusion.17
  34.0 0.0 copy-done
  34.0 0.0 copy-start.3
  34.0 0.0 copy-start.1
  34.1 4.4 fusion.3
  38.4 4.9 psum.22
  43.4 0.2 dynamic-update-slice
  43.6 61.0 %all-reduce = f32[4608]{0:T(1024)S(1)} all-reduce(f32[4608]{0:T(1024)S(1)} %dynamic-update-slice), channel_id=1, replica_groups=mesh['dp'=16,'tensor'=2] {'dp'}, use_global_device_ids=true, to_apply=%add | all-reduce | flops 4608 | bytes 36864
  104.6 0.0 copy-done.3
  104.6 0.1 fusion.11
  104.7 0.0 copy-done.1
  104.7 0.5 fusion.4
  105.2 4.3 fusion.19
  109.6 8.7 %all-reduce.2 = (bf16[320,16]{0,1:T(8,128)(2,1)S(1)}, bf16[320,16]{0,1:T(8,128)(2,1)S(1)}) all-reduce(f32[320,16]{0,1:T(8,128)S(1)} %fusion.19, f32[320,16]{0,1:T(8,128)S(1)} %fusion.4), channel_id=1, replica_groups=mesh['dp'=16,'tensor'=2] {'tensor'}, use_global_device_ids=true, to_apply=%region_1.0 | all-reduce | flops 10240 | bytes 61440 | tf_op jit(solution)/shard_map/psum | solution.py:15
  118.3 1.8 convolution_bitcast_fusion.1
  120.1 0.0 reduce-scatter.10.cloned.1.call-update
  120.1 0.0 reduce-scatter.12.cloned.1.call-start
  120.2 3.7 convolution_bitcast_fusion
  123.9 2.9 copy.14
  126.8 0.0 reduce-scatter.12.cloned.1.call-update
  126.8 0.0 reduce-scatter.8.cloned.1.call-start
  126.8 296.7 %all-gather.3.cloned.1.call-done = bf16[9216,4608]{0,1:T(8,128)(2,1)} async-done(((bf16[9216,288]{0,1:T(8,128)(2,1)}), bf16[9216,4608]{0,1:T(8,128)(2,1)}) %all-gather.3.cloned.1.call-update) | async-done | bytes 84934672 | tf_op jit(solution)/shard_map/all_gather | solution.py:21
  423.6 40.2 %fusion.18 = f32[320,4608]{1,0:T(8,128)} fusion(bf16[320,9216]{1,0:T(8,128)(2,1)} %param.6, bf16[9216,4608]{0,1:T(8,128)(2,1)} %all-gather.3.cloned.1.call-done), kind=kOutput, calls=%fused_computation.24 | convolution fusion | flops 27179089920 | bytes 96731136 | tf_op jit(solution)/shard_map/dot_general | solution.py:23
  463.8 0.0 reduce-scatter.8.cloned.1.call-update
  464.4 22.3 %reduce-scatter.10.cloned.1.call-done = f32[144,16]{1,0:T(8,128)} async-done(((f32[2304,16]{1,0:T(8,128)}), f32[144,16]{1,0:T(8,128)}) %reduce-scatter.10.cloned.1.call-update) | async-done | bytes 9232
  486.7 1.6 copy.13
  488.3 77.0 %reduce-scatter.12.cloned.1.call-done = f32[576,16]{1,0:T(8,128)} async-done(((f32[9216,16]{1,0:T(8,128)}), f32[576,16]{1,0:T(8,128)}) %reduce-scatter.12.cloned.1.call-update) | async-done | bytes 36880
  565.2 1.7 copy.15
  566.9 72.6 %reduce-scatter.8.cloned.1.call-done = f32[320,2304]{1,0:T(8,128)} async-done(((f32[320,4608]{1,0:T(8,128)}), f32[320,2304]{1,0:T(8,128)}) %reduce-scatter.8.cloned.1.call-update) | async-done | bytes 2949136 | tf_op jit(solution)/shard_map/reduce_scatter | solution.py:30
  639.6 3.7 fusion.1
  643.3 0.1 fusion.12
  643.3 61.0 %all-reduce.1 = f32[2304]{0:T(1024)S(1)} all-reduce(f32[2304]{0:T(1024)S(1)} %fusion.12), channel_id=3, replica_groups=mesh['dp'=16,'tensor'=2] {'dp'}, use_global_device_ids=true, to_apply=%region_5.0.clone | all-reduce | flops 2304 | bytes 18432
  704.4 0.6 dynamic-slice.3
  (2 shorter events, 0.0 us)
Async XLA Ops:
  7.2 26.9 %copy-start = (bf16[9216,16]{0,1:T(8,128)(2,1)S(1)}, bf16[9216,16]{0,1:T(8,128)(2,1)}, u32[]{:S(2)}) copy-start(bf16[9216,16]{0,1:T(8,128)(2,1)} %param.8) | copy-start | bytes 884740
  7.2 25.6 %copy-start.4 = (u32[32]{0:T(128)S(1)}, u32[32]{0:T(128)}, u32[]{:S(2)}) copy-start(u32[32]{0:T(128)} %constant.16) | copy-start | bytes 388
  7.2 0.8 copy-start.2
  7.2 416.4 %all-gather.3.cloned.1.call-start = ((), (), s32[]{:S(2)}) async-start(), calls=%async_computation.3 | async-start | bytes 90243072 | tf_op jit(solution)/shard_map/all_gather | solution.py:21
  7.9 478.8 %reduce-scatter.10.cloned.1.call-start = ((), (), s32[]{:S(2)}) async-start(), calls=%async_computation.5 | async-start | bytes 1253376
  34.0 70.6 %copy-start.3 = (f32[2304]{0:T(1024)S(1)}, f32[2304]{0:T(1024)}, u32[]{:S(2)}) copy-start(f32[2304]{0:T(1024)} %param.10) | copy-start | bytes 27652
  34.0 70.7 %copy-start.1 = (bf16[320,2304]{1,0:T(8,128)(2,1)S(1)}, bf16[320,2304]{1,0:T(8,128)(2,1)}, u32[]{:S(2)}) copy-start(bf16[320,2304]{1,0:T(8,128)(2,1)} %param.11) | copy-start | bytes 4423684
  120.1 445.1 %reduce-scatter.12.cloned.1.call-start = ((), (), s32[]{:S(2)}) async-start(), calls=%async_computation.6 | async-start | bytes 5013504
  126.8 512.8 %reduce-scatter.8.cloned.1.call-start = ((), (), s32[]{:S(2)}) async-start(), calls=%async_computation.4 | async-start | bytes 8847360 | tf_op jit(solution)/shard_map/reduce_scatter | solution.py:30
Sparse Core Ops, SparseCore 0:
  9.6 413.9 all-gather.2
  427.7 58.9 reduce-scatter.9
  490.6 74.6 reduce-scatter.11
  567.4 72.1 reduce-scatter.7
where the time goes:
time: 712 us
  waiting for transfers between devices  469 us (66%)
  blocking collectives  160 us (22%)
  matrix products  58.6 us (8%)
  between operations  15.2 us (2%)
  local copies, waits for them, and re-layouts  7.9 us (1%)
    all_gather x1, waiting for transfers between devices, body(): w_piece = lax.all_gather(fixed_down_weight, 'dp', axis=1, tiled=True)  297 us
    unnamed x2, blocking collectives  122 us
    unnamed x6, waiting for transfers between devices  100 us
    reduce_scatter x1, waiting for transfers between devices, body(): lax.psum_scatter(products, 'tensor', scatter_dimension=1, tiled=True)  72.6 us
    dot_general x1, matrix products, body(): products = jnp.dot(hidden, w_piece, preferred_element_type=jnp.float32)  40.2 us
    all_gather x1, blocking collectives, body(): factor_a_slice = lax.all_gather(lowrank_factor_a, 'dp', axis=1, tiled=True)  24.5 us
  transfers between devices with their start and end apart: 4, of which 4 were waited for; matrix products, arithmetic and copies ran while one was open for 9% of the time, Pallas kernels for 0%

commit v1 on v0

--- a/solution.py
+++ b/solution.py
@@ -2,6 +2,24 @@
 import jax.numpy as jnp
 from jax import lax
 from jax.sharding import PartitionSpec as P
+
+
+def ring_gather(value, axis, dim):
+    ways, here, turn = (lax.axis_size(axis), lax.axis_index(axis), value.shape[dim])
+    shape = [n * ways if d == dim else n for d, n in enumerate(value.shape)]
+    full = lax.dynamic_update_slice_in_dim(
+        jnp.zeros(shape, value.dtype), value, here * turn, axis=dim
+    )
+    going_up = going_down = value
+    for far in range(1, ways // 2 + 1):
+        going_up = lax.ppermute(going_up, axis, [(d, (d + 1) % ways) for d in range(ways)])
+        full = lax.dynamic_update_slice_in_dim(full, going_up, (here - far) % ways * turn, axis=dim)
+        if 2 * far < ways:
+            going_down = lax.ppermute(going_down, axis, [(d, (d - 1) % ways) for d in range(ways)])
+            full = lax.dynamic_update_slice_in_dim(
+                full, going_down, (here + far) % ways * turn, axis=dim
+            )
+    return full
 
 
 def body(hidden, fixed_down_weight, lowrank_factor_b, lowrank_factor_a, magnitude, cotangent):
@@ -18,7 +36,7 @@
     weight_shape = (1, 1)
     squares = jnp.zeros((sq_len,), jnp.float32)
     full_w = jnp.zeros(weight_shape, jnp.bfloat16)
-    w_piece = lax.all_gather(fixed_down_weight, "dp", axis=1, tiled=True)
+    w_piece = ring_gather(fixed_down_weight, "dp", 1)
     factor_a_slice = lax.all_gather(lowrank_factor_a, "dp", axis=1, tiled=True)
     products = jnp.dot(hidden, w_piece, preferred_element_type=jnp.float32)
     full_a = factor_a_slice

time: 712 us -> 1180 us (1.66)
  starting transfers between devices: 0.16 us -> 532 us
  waiting for transfers between devices: 469 us -> 265 us
  local copies, waits for them, and re-layouts: 7.9 us -> 103 us
  blocking collectives: 160 us -> 206 us
    ppermute x0 -> x15, starting transfers between devices: none -> 532 us  [the longest x8 517 us: ring_gather(): lax.ppermute(going_up, axis, [(d, (d + 1) % ways) for d in range(ways)])]
    all_gather x1 -> x0, waiting for transfers between devices: 297 us -> none  [body(): w_piece = lax.all_gather(fixed_down_weight, 'dp', axis=1, tiled=True)]
    ppermute x0 -> x15, waiting for transfers between devices: none -> 162 us  [the longest x8 162 us: ring_gather(): lax.ppermute(going_up, axis, [(d, (d + 1) % ways) for d in range(ways)])]
    unnamed x6 -> x5, waiting for transfers between devices: 100 us -> 0.07 us
    dynamic_update_slice x0 -> x16, local copies, waits for them, and re-layouts: none -> 64.3 us  [the longest x8 32.4 us: ring_gather(): lax.dynamic_update_slice_in_dim(full, going_up, (here - far) % ways * tur...]
    all_gather x1, blocking collectives: 24.5 us -> 73.3 us  [body(): factor_a_slice = lax.all_gather(lowrank_factor_a, 'dp', axis=1, tiled=True)]
    reduce_scatter x1, waiting for transfers between devices: 72.6 us -> 103 us  [body(): lax.psum_scatter(products, 'tensor', scatter_dimension=1, tiled=True)]
    broadcast_in_dim x0 -> x1, local copies, waits for them, and re-layouts: none -> 27.8 us  [ring_gather(): jnp.zeros(shape, value.dtype)]
  transfers between devices with their start and end apart: 4 -> 18, of which waited for: 4 -> 8; matrix products, arithmetic and copies ran while one was open for 9% -> 13% of each run, Pallas kernels for 0% -> 0%
where the time goes in v1:
time: 1180 us
  starting transfers between devices  532 us (45%)
  waiting for transfers between devices  265 us (22%)
  blocking collectives  206 us (17%)
  local copies, waits for them, and re-layouts  103 us (9%)
  matrix products  56.3 us (5%)
  between operations  15.6 us (1%)
    ppermute x8, starting transfers between devices, ring_gather(): lax.ppermute(going_up, axis, [(d, (d + 1) % ways) for d in range(ways)])  517 us
    ppermute x8, waiting for transfers between devices, ring_gather(): lax.ppermute(going_up, axis, [(d, (d + 1) % ways) for d in range(ways)])  162 us
    unnamed x2, blocking collectives  119 us
    reduce_scatter x1, waiting for transfers between devices, body(): lax.psum_scatter(products, 'tensor', scatter_dimension=1, tiled=True)  103 us
    all_gather x1, blocking collectives, body(): factor_a_slice = lax.all_gather(lowrank_factor_a, 'dp', axis=1, tiled=True)  73.3 us
    dot_general x1, matrix products, body(): products = jnp.dot(hidden, w_piece, preferred_element_type=jnp.float32)  41.1 us
    dynamic_update_slice x8, local copies, waits for them, and re-layouts, ring_gather(): lax.dynamic_update_slice_in_dim(full, going_up, (here - far) % ways * tur...  32.4 us
    dynamic_update_slice x7, local copies, waits for them, and re-layouts, ring_gather(): lax.dynamic_update_slice_in_dim(full, going_down, (here + far) % ways * t...  29.2 us
  transfers between devices with their start and end apart: 18, of which 8 were waited for; matrix products, arithmetic and copies ran while one was open for 13% of the time, Pallas kernels for 0%

profile of v1, /device:TPU:0, one launch (start us, length us, event | category | flops | bytes accessed | tf_op | source)
XLA Modules:
  0.0 1182.2 jit_solution(4994721848121186545)
XLA Ops:
  7.2 0.0 reduce-scatter.10.cloned.1.call-start
  7.2 0.5 collective-permute-start
  7.8 5.0 collective-permute-start.1
  12.8 58.4 %collective-permute-done = bf16[9216,288]{0,1:T(8,128)(2,1)S(1)} collective-permute-done((bf16[9216,288]{0,1:T(8,128)(2,1)}, bf16[9216,288]{0,1:T(8,128)(2,1)S(1)}, u32[]{:S(2)}, u32[]{:S(2)}) %collective-permute-start) | collective-permute-done | bytes 5308448 | tf_op jit(solution)/shard_map/ppermute | solution.py:15
  71.2 53.8 %collective-permute-start.2 = (bf16[9216,288]{0,1:T(8,128)(2,1)S(1)}, bf16[9216,288]{0,1:T(8,128)(2,1)S(1)}, u32[]{:S(2)}, u32[]{:S(2)}) collective-permute-start(bf16[9216,288]{0,1:T(8,128)(2,1)S(1)} %collective-permute-done), channel_id=1, source_target_pairs={{0,2},{2,4},{4,6},{6,8},{8,10},{10,12},{12,14},{14,16},{16,18},{18... | collective-permute-start | bytes 15925256 | tf_op jit(solution)/shard_map/ppermute | solution.py:15
  125.0 8.9 collective-permute-done.2
  133.8 107.1 %collective-permute-start.4 = (bf16[9216,288]{0,1:T(8,128)(2,1)S(1)}, bf16[9216,288]{0,1:T(8,128)(2,1)S(1)}, u32[]{:S(2)}, u32[]{:S(2)}) collective-permute-start(bf16[9216,288]{0,1:T(8,128)(2,1)S(1)} %collective-permute-done.2), channel_id=1, source_target_pairs={{0,2},{2,4},{4,6},{6,8},{8,10},{10,12},{12,14},{14,16},{16,18},{18... | collective-permute-start | bytes 15925256 | tf_op jit(solution)/shard_map/ppermute | solution.py:15
  240.9 8.4 collective-permute-done.4
  249.3 2.3 copy-done.3
  251.6 107.6 %collective-permute-start.6 = (bf16[9216,288]{0,1:T(8,128)(2,1)S(1)}, bf16[9216,288]{0,1:T(8,128)(2,1)}, u32[]{:S(2)}, u32[]{:S(2)}) collective-permute-start(bf16[9216,288]{0,1:T(8,128)(2,1)S(1)} %collective-permute-done.4), channel_id=1, source_target_pairs={{0,2},{2,4},{4,6},{6,8},{8,10},{10,12},{12,14},{14,16},{16,18},{18... | collective-permute-start | bytes 15925256 | tf_op jit(solution)/shard_map/ppermute | solution.py:15
  359.2 8.5 collective-permute-done.6
  367.8 107.7 %collective-permute-start.8 = (bf16[9216,288]{0,1:T(8,128)(2,1)}, bf16[9216,288]{0,1:T(8,128)(2,1)}, u32[]{:S(2)}, u32[]{:S(2)}) collective-permute-start(bf16[9216,288]{0,1:T(8,128)(2,1)} %collective-permute-done.6), channel_id=1, source_target_pairs={{0,2},{2,4},{4,6},{6,8},{8,10},{10,12},{12,14},{14,16},{16,18},{18... | collective-permute-start | bytes 15925256 | tf_op jit(solution)/shard_map/ppermute | solution.py:15
  475.4 73.3 %all-gather = bf16[16,288,16]{1,2,0:T(8,128)(2,1)S(1)} all-gather(bf16[1,288,16]{1,2,0:T(8,128)(2,1)} %bitcast.34), channel_id=1, replica_groups=mesh['dp'=16,'tensor'=2] {'dp'}, dimensions={0}, use_global_device_ids=true | all-gather | bytes 156672 | tf_op jit(solution)/shard_map/all_gather | solution.py:40
  548.8 0.2 reshape.13
  549.0 1.3 fusion.18
  551.0 4.3 fusion.3
  555.3 5.1 psum.22
  560.3 0.2 dynamic-update-slice
  560.6 57.6 %all-reduce = f32[4608]{0:T(1024)S(1)} all-reduce(f32[4608]{0:T(1024)S(1)} %dynamic-update-slice), channel_id=1, replica_groups=mesh['dp'=16,'tensor'=2] {'dp'}, use_global_device_ids=true, to_apply=%add | all-reduce | flops 4608 | bytes 36864
  618.2 0.1 fusion.12
  618.3 4.3 fusion.19
  622.6 0.0 collective-permute-start.9
  622.6 0.5 fusion.4
  623.1 8.6 all-reduce.2
  631.8 1.8 convolution_bitcast_fusion.2
  633.6 0.0 reduce-scatter.12.cloned.1.call-start
  633.7 3.7 convolution_bitcast_fusion
  637.4 3.0 copy.14
  640.5 0.0 reduce-scatter.8.cloned.1.call-start
  640.8 0.1 collective-permute-start.10
  640.9 27.8 %broadcast_in_dim.2 = bf16[9216,4608]{0,1:T(8,128)(2,1)} broadcast(bf16[]{:T(256)} %constant.95.clone.1), dimensions={} | broadcast | bytes 84934656 | tf_op jit(solution)/shard_map/broadcast_in_dim | solution.py:11
  668.7 2.7 constant_dynamic-update-slice_fusion.15
  671.4 5.7 constant_dynamic-update-slice_fusion.14
  677.1 5.5 constant_dynamic-update-slice_fusion.13
  682.6 3.0 constant_dynamic-update-slice_fusion.12
  685.7 3.0 collective-permute-start.11
  688.6 2.7 constant_dynamic-update-slice_fusion.11
  691.3 17.2 %collective-permute-done.10 = bf16[9216,288]{0,1:T(8,128)(2,1)} collective-permute-done((bf16[9216,288]{0,1:T(8,128)(2,1)}, bf16[9216,288]{0,1:T(8,128)(2,1)}, u32[]{:S(2)}, u32[]{:S(2)}) %collective-permute-start.10) | collective-permute-done | bytes 5308448 | tf_op jit(solution)/shard_map/ppermute | solution.py:15
  708.5 83.3 %collective-permute-start.12 = (bf16[9216,288]{0,1:T(8,128)(2,1)}, bf16[9216,288]{0,1:T(8,128)(2,1)S(1)}, u32[]{:S(2)}, u32[]{:S(2)}) collective-permute-start(bf16[9216,288]{0,1:T(8,128)(2,1)} %collective-permute-done.10), channel_id=1, source_target_pairs={{0,2},{2,4},{4,6},{6,8},{8,10},{10,12},{12,14},{14,16},{16,18},{18... | collective-permute-start | bytes 15925256 | tf_op jit(solution)/shard_map/ppermute | solution.py:15
  791.8 2.7 constant_dynamic-update-slice_fusion.10
  794.5 5.2 constant_dynamic-update-slice_fusion.9
  799.7 5.2 constant_dynamic-update-slice_fusion.8
  804.9 5.2 constant_dynamic-update-slice_fusion.7
  810.1 7.2 collective-permute-start.13
  817.3 5.2 constant_dynamic-update-slice_fusion.6
  822.6 45.4 %collective-permute-done.12 = bf16[9216,288]{0,1:T(8,128)(2,1)S(1)} collective-permute-done((bf16[9216,288]{0,1:T(8,128)(2,1)}, bf16[9216,288]{0,1:T(8,128)(2,1)S(1)}, u32[]{:S(2)}, u32[]{:S(2)}) %collective-permute-start.12) | collective-permute-done | bytes 5308448 | tf_op jit(solution)/shard_map/ppermute | solution.py:15
  868.0 56.6 %collective-permute-start.14 = (bf16[9216,288]{0,1:T(8,128)(2,1)S(1)}, bf16[9216,288]{0,1:T(8,128)(2,1)S(1)}, u32[]{:S(2)}, u32[]{:S(2)}) collective-permute-start(bf16[9216,288]{0,1:T(8,128)(2,1)S(1)} %collective-permute-done.12), channel_id=1, source_target_pairs={{0,2},{2,4},{4,6},{6,8},{8,10},{10,12},{12,14},{14,16},{16,18},{18... | collective-permute-start | bytes 15925256 | tf_op jit(solution)/shard_map/ppermute | solution.py:15
  924.6 5.2 constant_dynamic-update-slice_fusion.5
  929.9 5.1 constant_dynamic-update-slice_fusion.4
  935.0 2.7 constant_dynamic-update-slice_fusion.3
  937.8 2.6 constant_dynamic-update-slice_fusion.2
  940.4 2.7 constant_dynamic-update-slice_fusion.1
  943.1 15.5 %collective-permute-done.14 = bf16[9216,288]{0,1:T(8,128)(2,1)S(1)} collective-permute-done((bf16[9216,288]{0,1:T(8,128)(2,1)S(1)}, bf16[9216,288]{0,1:T(8,128)(2,1)S(1)}, u32[]{:S(2)}, u32[]{:S(2)}) %collective-permute-start.14) | collective-permute-done | bytes 5308448 | tf_op jit(solution)/shard_map/ppermute | solution.py:15
  958.6 2.8 constant_dynamic-update-slice_fusion
  961.3 41.1 %convolution_bitcast_fusion.1 = f32[320,4608]{1,0:T(8,128)} fusion(bf16[9216,4608]{0,1:T(8,128)(2,1)} %constant_dynamic-update-slice_fusion, bf16[320,9216]{1,0:T(8,128)(2,1)} %param.6), kind=kOutput, calls=%fused_computation.3 | convolution fusion | flops 27179089920 | bytes 96731136 | tf_op jit(solution)/shard_map/dot_general | solution.py:41
  1003.1 0.6 fusion.7
  1003.7 0.0 reduce-scatter.10.cloned.1.call-done
  1003.7 1.6 copy.13
  1005.3 1.7 copy.15
  1007.0 103.0 %reduce-scatter.8.cloned.1.call-done = f32[320,2304]{1,0:T(8,128)} async-done(((f32[320,4608]{1,0:T(8,128)}), f32[320,2304]{1,0:T(8,128)}) %reduce-scatter.8.cloned.1.call-update) | async-done | bytes 2949136 | tf_op jit(solution)/shard_map/reduce_scatter | solution.py:48
  1110.0 3.9 fusion.1
  1113.9 0.1 fusion.13
  1114.0 61.0 %all-reduce.1 = f32[2304]{0:T(1024)S(1)} all-reduce(f32[2304]{0:T(1024)S(1)} %fusion.13), channel_id=3, replica_groups=mesh['dp'=16,'tensor'=2] {'dp'}, use_global_device_ids=true, to_apply=%region_5.6.clone | all-reduce | flops 2304 | bytes 18432
  1175.0 0.6 dynamic-slice.3
  (54 shorter events, 0.2 us)
Async XLA Ops:
  7.2 543.8 %copy-start = (bf16[9216,16]{0,1:T(8,128)(2,1)S(1)}, bf16[9216,16]{0,1:T(8,128)(2,1)}, u32[]{:S(2)}) copy-start(bf16[9216,16]{0,1:T(8,128)(2,1)} %param.8) | copy-start | bytes 884740
  7.2 996.6 %reduce-scatter.10.cloned.1.call-start = ((), (), s32[]{:S(2)}) async-start(), calls=%async_computation.4 | async-start | bytes 1253376
  7.2 63.9 %collective-permute-start = (bf16[9216,288]{0,1:T(8,128)(2,1)}, bf16[9216,288]{0,1:T(8,128)(2,1)S(1)}, u32[]{:S(2)}, u32[]{:S(2)}) collective-permute-start(bf16[9216,288]{0,1:T(8,128)(2,1)} %param.7), channel_id=1, source_target_pairs={{0,2},{2,4},{4,6},{6,8},{8,10},{10,12},{12,14},{14,16},{16,18},{18... | collective-permute-start | bytes 15925256 | tf_op jit(solution)/shard_map/ppermute | solution.py:15
  7.8 117.2 %collective-permute-start.1 = (bf16[9216,288]{0,1:T(8,128)(2,1)}, bf16[9216,288]{0,1:T(8,128)(2,1)S(1)}, u32[]{:S(2)}, u32[]{:S(2)}) collective-permute-start(bf16[9216,288]{0,1:T(8,128)(2,1)} %param.7), channel_id=1, source_target_pairs={{0,30},{2,0},{4,2},{6,4},{8,6},{10,8},{12,10},{14,12},{16,14},{18,... | collective-permute-start | bytes 15925256 | tf_op jit(solution)/shard_map/ppermute | solution.py:18
  71.2 53.8 %copy-start.5 = (bf16[9216,288]{0,1:T(8,128)(2,1)}, bf16[9216,288]{0,1:T(8,128)(2,1)S(1)}, u32[]{:S(2)}) copy-start(bf16[9216,288]{0,1:T(8,128)(2,1)S(1)} %collective-permute-done) | copy-start | bytes 15925252
  71.2 62.7 %collective-permute-start.2 = (bf16[9216,288]{0,1:T(8,128)(2,1)S(1)}, bf16[9216,288]{0,1:T(8,128)(2,1)S(1)}, u32[]{:S(2)}, u32[]{:S(2)}) collective-permute-start(bf16[9216,288]{0,1:T(8,128)(2,1)S(1)} %collective-permute-done), channel_id=1, source_target_pairs={{0,2},{2,4},{4,6},{6,8},{8,10},{10,12},{12,14},{14,16},{16,18},{18... | collective-permute-start | bytes 15925256 | tf_op jit(solution)/shard_map/ppermute | solution.py:15
  124.9 350.5 %copy-start.6 = (bf16[9216,288]{0,1:T(8,128)(2,1)}, bf16[9216,288]{0,1:T(8,128)(2,1)S(1)}, u32[]{:S(2)}) copy-start(bf16[9216,288]{0,1:T(8,128)(2,1)S(1)} %collective-permute-done.1) | copy-start | bytes 15925252
  125.0 116.0 %collective-permute-start.3 = (bf16[9216,288]{0,1:T(8,128)(2,1)S(1)}, bf16[9216,288]{0,1:T(8,128)(2,1)S(1)}, u32[]{:S(2)}, u32[]{:S(2)}) collective-permute-start(bf16[9216,288]{0,1:T(8,128)(2,1)S(1)} %collective-permute-done.1), channel_id=1, source_target_pairs={{0,30},{2,0},{4,2},{6,4},{8,6},{10,8},{12,10},{14,12},{16,14},{18,... | collective-permute-start | bytes 15925256 | tf_op jit(solution)/shard_map/ppermute | solution.py:18
  133.8 341.6 %copy-start.7 = (bf16[9216,288]{0,1:T(8,128)(2,1)}, bf16[9216,288]{0,1:T(8,128)(2,1)S(1)}, u32[]{:S(2)}) copy-start(bf16[9216,288]{0,1:T(8,128)(2,1)S(1)} %collective-permute-done.2) | copy-start | bytes 15925252
  133.8 115.5 %collective-permute-start.4 = (bf16[9216,288]{0,1:T(8,128)(2,1)S(1)}, bf16[9216,288]{0,1:T(8,128)(2,1)S(1)}, u32[]{:S(2)}, u32[]{:S(2)}) collective-permute-start(bf16[9216,288]{0,1:T(8,128)(2,1)S(1)} %collective-permute-done.2), channel_id=1, source_target_pairs={{0,2},{2,4},{4,6},{6,8},{8,10},{10,12},{12,14},{14,16},{16,18},{18... | collective-permute-start | bytes 15925256 | tf_op jit(solution)/shard_map/ppermute | solution.py:15
  240.9 126.8 %copy-start.4 = (bf16[9216,288]{0,1:T(8,128)(2,1)}, bf16[9216,288]{0,1:T(8,128)(2,1)S(1)}, u32[]{:S(2)}) copy-start(bf16[9216,288]{0,1:T(8,128)(2,1)S(1)} %collective-permute-done.3) | copy-start | bytes 15925252
  240.9 118.3 %collective-permute-start.5 = (bf16[9216,288]{0,1:T(8,128)(2,1)S(1)}, bf16[9216,288]{0,1:T(8,128)(2,1)}, u32[]{:S(2)}, u32[]{:S(2)}) collective-permute-start(bf16[9216,288]{0,1:T(8,128)(2,1)S(1)} %collective-permute-done.3), channel_id=1, source_target_pairs={{0,30},{2,0},{4,2},{6,4},{8,6},{10,8},{12,10},{14,12},{16,14},{18,... | collective-permute-start | bytes 15925256 | tf_op jit(solution)/shard_map/ppermute | solution.py:18
  249.3 2.3 copy-start.3
  251.6 116.1 %collective-permute-start.6 = (bf16[9216,288]{0,1:T(8,128)(2,1)S(1)}, bf16[9216,288]{0,1:T(8,128)(2,1)}, u32[]{:S(2)}, u32[]{:S(2)}) collective-permute-start(bf16[9216,288]{0,1:T(8,128)(2,1)S(1)} %collective-permute-done.4), channel_id=1, source_target_pairs={{0,2},{2,4},{4,6},{6,8},{8,10},{10,12},{12,14},{14,16},{16,18},{18... | collective-permute-start | bytes 15925256 | tf_op jit(solution)/shard_map/ppermute | solution.py:15
  359.2 263.3 %collective-permute-start.7 = (bf16[9216,288]{0,1:T(8,128)(2,1)}, bf16[9216,288]{0,1:T(8,128)(2,1)}, u32[]{:S(2)}, u32[]{:S(2)}) collective-permute-start(bf16[9216,288]{0,1:T(8,128)(2,1)} %collective-permute-done.5), channel_id=1, source_target_pairs={{0,30},{2,0},{4,2},{6,4},{8,6},{10,8},{12,10},{14,12},{16,14},{18,... | collective-permute-start | bytes 15925256 | tf_op jit(solution)/shard_map/ppermute | solution.py:18
  367.8 273.1 %collective-permute-start.8 = (bf16[9216,288]{0,1:T(8,128)(2,1)}, bf16[9216,288]{0,1:T(8,128)(2,1)}, u32[]{:S(2)}, u32[]{:S(2)}) collective-permute-start(bf16[9216,288]{0,1:T(8,128)(2,1)} %collective-permute-done.6), channel_id=1, source_target_pairs={{0,2},{2,4},{4,6},{6,8},{8,10},{10,12},{12,14},{14,16},{16,18},{18... | collective-permute-start | bytes 15925256 | tf_op jit(solution)/shard_map/ppermute | solution.py:15
  551.0 67.2 %copy-start.8 = (f32[2304]{0:T(1024)S(1)}, f32[2304]{0:T(1024)}, u32[]{:S(2)}) copy-start(f32[2304]{0:T(1024)} %param.10) | copy-start | bytes 27652
  555.3 67.4 %copy-start.2 = (bf16[320,2304]{1,0:T(8,128)(2,1)S(1)}, bf16[320,2304]{1,0:T(8,128)(2,1)}, u32[]{:S(2)}) copy-start(bf16[320,2304]{1,0:T(8,128)(2,1)} %param.11) | copy-start | bytes 4423684
  622.6 63.1 %collective-permute-start.9 = (bf16[9216,288]{0,1:T(8,128)(2,1)}, bf16[9216,288]{0,1:T(8,128)(2,1)}, u32[]{:S(2)}, u32[]{:S(2)}) collective-permute-start(bf16[9216,288]{0,1:T(8,128)(2,1)} %collective-permute-done.7), channel_id=1, source_target_pairs={{0,30},{2,0},{4,2},{6,4},{8,6},{10,8},{12,10},{14,12},{16,14},{18,... | collective-permute-start | bytes 15925256 | tf_op jit(solution)/shard_map/ppermute | solution.py:18
  633.6 371.7 %reduce-scatter.12.cloned.1.call-start = ((), (), s32[]{:S(2)}) async-start(), calls=%async_computation.5 | async-start | bytes 5013504
  640.5 469.5 %reduce-scatter.8.cloned.1.call-start = ((), (), s32[]{:S(2)}) async-start(), calls=%async_computation.3 | async-start | bytes 8847360 | tf_op jit(solution)/shard_map/reduce_scatter | solution.py:48
  640.8 27.9 %slice-start = ((s8[5308416]{0:T(1024)(128)(4,1)}), s8[1114112]{0:T(1024)(128)(4,1)S(1)}, s32[]{:S(2)}) async-start(s8[5308416]{0:T(1024)(128)(4,1)} %bitcast.25), calls=%async_computation.6 | async-start | bytes 2228224
  640.8 27.9 %slice-start.1 = ((s8[5308416]{0:T(1024)(128)(4,1)}), s8[4194304]{0:T(1024)(128)(4,1)S(1)}, s32[]{:S(2)}) async-start(s8[5308416]{0:T(1024)(128)(4,1)} %bitcast.25), calls=%async_computation.7 | async-start | bytes 8388608
  640.8 67.7 %collective-permute-start.10 = (bf16[9216,288]{0,1:T(8,128)(2,1)}, bf16[9216,288]{0,1:T(8,128)(2,1)}, u32[]{:S(2)}, u32[]{:S(2)}) collective-permute-start(bf16[9216,288]{0,1:T(8,128)(2,1)} %collective-permute-done.8), channel_id=1, source_target_pairs={{0,2},{2,4},{4,6},{6,8},{8,10},{10,12},{12,14},{14,16},{16,18},{18... | collective-permute-start | bytes 15925256 | tf_op jit(solution)/shard_map/ppermute | solution.py:15
  671.4 11.2 slice-start.6
  671.4 17.2 %slice-start.4 = ((s8[5308416]{0:T(1024)(128)(4,1)}), s8[4194304]{0:T(1024)(128)(4,1)S(1)}, s32[]{:S(2)}) async-start(s8[5308416]{0:T(1024)(128)(4,1)} %bitcast.29), calls=%async_computation.10 | async-start | bytes 8388608
  677.1 5.5 slice-start.7
  677.1 11.5 slice-start.5
  682.6 109.2 %slice-start.2 = ((s8[5308416]{0:T(1024)(128)(4,1)}), s8[4194304]{0:T(1024)(128)(4,1)S(1)}, s32[]{:S(2)}) async-start(s8[5308416]{0:T(1024)(128)(4,1)} %bitcast.27), calls=%async_computation.8 | async-start | bytes 8388608
  685.7 106.1 %slice-start.3 = ((s8[5308416]{0:T(1024)(128)(4,1)}), s8[1114112]{0:T(1024)(128)(4,1)S(1)}, s32[]{:S(2)}) async-start(s8[5308416]{0:T(1024)(128)(4,1)} %bitcast.27), calls=%async_computation.9 | async-start | bytes 2228224
  685.7 124.4 %collective-permute-start.11 = (bf16[9216,288]{0,1:T(8,128)(2,1)}, bf16[9216,288]{0,1:T(8,128)(2,1)S(1)}, u32[]{:S(2)}, u32[]{:S(2)}) collective-permute-start(bf16[9216,288]{0,1:T(8,128)(2,1)} %collective-permute-done.9), channel_id=1, source_target_pairs={{0,30},{2,0},{4,2},{6,4},{8,6},{10,8},{12,10},{14,12},{16,14},{18,... | collective-permute-start | bytes 15925256 | tf_op jit(solution)/shard_map/ppermute | solution.py:18
  708.5 159.5 %collective-permute-start.12 = (bf16[9216,288]{0,1:T(8,128)(2,1)}, bf16[9216,288]{0,1:T(8,128)(2,1)S(1)}, u32[]{:S(2)}, u32[]{:S(2)}) collective-permute-start(bf16[9216,288]{0,1:T(8,128)(2,1)} %collective-permute-done.10), channel_id=1, source_target_pairs={{0,2},{2,4},{4,6},{6,8},{8,10},{10,12},{12,14},{14,16},{16,18},{18... | collective-permute-start | bytes 15925256 | tf_op jit(solution)/shard_map/ppermute | solution.py:15
  810.1 130.3 %collective-permute-start.13 = (bf16[9216,288]{0,1:T(8,128)(2,1)S(1)}, bf16[9216,288]{0,1:T(8,128)(2,1)S(1)}, u32[]{:S(2)}, u32[]{:S(2)}) collective-permute-start(bf16[9216,288]{0,1:T(8,128)(2,1)S(1)} %collective-permute-done.11), channel_id=1, source_target_pairs={{0,30},{2,0},{4,2},{6,4},{8,6},{10,8},{12,10},{14,12},{16,14},{18,... | collective-permute-start | bytes 15925256 | tf_op jit(solution)/shard_map/ppermute | solution.py:18
  868.0 90.6 %collective-permute-start.14 = (bf16[9216,288]{0,1:T(8,128)(2,1)S(1)}, bf16[9216,288]{0,1:T(8,128)(2,1)S(1)}, u32[]{:S(2)}, u32[]{:S(2)}) collective-permute-start(bf16[9216,288]{0,1:T(8,128)(2,1)S(1)} %collective-permute-done.12), channel_id=1, source_target_pairs={{0,2},{2,4},{4,6},{6,8},{8,10},{10,12},{12,14},{14,16},{16,18},{18... | collective-permute-start | bytes 15925256 | tf_op jit(solution)/shard_map/ppermute | solution.py:15
  1002.4 173.2 %copy-start.1 = (bf16[9216,16]{0,1:T(8,128)(2,1)S(1)}, bf16[9216,16]{0,1:T(8,128)(2,1)}, u32[]{:S(2)}) copy-start(bf16[9216,16]{0,1:T(8,128)(2,1)} %param.8) | copy-start | bytes 884740
Sparse Core Ops, SparseCore 0:
  633.8 137.6 reduce-scatter.9
  775.3 141.6 reduce-scatter.11
  1002.6 107.4 reduce-scatter.7
